TPU v7x, 32 devices: a whole 2x2x4 slice. The times are simulated.
32 devices in a mesh: row: 4 (over y, core), col: 8 (over z, x).
Axes of the slice: x: 2, y: 2, z: 4, core: 2. Of those that a mesh axis runs over, the one named last changes fastest.
Arguments:
- velocity_modes: bfloat16 [3, 176, 352, 704], P(None, 'row', 'col'), may hold values from -0.00090789795 to 0.00090789795
- wavenumbers: float32 [8], replicated, may hold values from 0.5 to 3
- polar: float32 [8], replicated, may hold values from -3.140625 to 3.140625
- azimuth: float32 [8], replicated, may hold values from -3.140625 to 3.140625
Outputs:
- velocity: bfloat16 [3, 512, 512, 512], P(None, 'row', 'col')
- far_field: float32 [8, 2, 8], P('col')
All inputs are finite; a program needn't handle non-finite values.
Results may differ from a plain program's by a relative error of at most 0.0075.
Values may be sent and summed in bfloat16 or wider, within the bound.
A program may use at most 192 MiB of HBM per device.

v0:
```python
import math
import jax
import jax.numpy as jnp
from jax import lax
from jax.sharding import PartitionSpec as P

N = 512
M = 352
KX = 176
FREQS = 8


def complex_table(modes, points):
    waves = jnp.arange(modes, dtype=jnp.int32) - modes // 2
    cells = jnp.arange(points, dtype=jnp.int32)
    product = jnp.mod(waves[:, None] * cells[None, :], points)
    angle = product.astype(jnp.float32) * (2.0 * math.pi / points)
    cosine = jnp.cos(angle)
    sine = jnp.sin(angle)
    table = jnp.stack([jnp.stack([cosine, sine], 1), jnp.stack([-sine, cosine], 1)], 0)
    return table.astype(jnp.bfloat16)


def half_table(count, points):
    waves = jnp.arange(count, dtype=jnp.int32)
    cells = jnp.arange(points, dtype=jnp.int32)
    product = jnp.mod(waves[:, None] * cells[None, :], points)
    angle = product.astype(jnp.float32) * (2.0 * math.pi / points)
    cosine = jnp.cos(angle).astype(jnp.bfloat16)
    sine = jnp.sin(angle).astype(jnp.bfloat16)
    factor = jnp.where(waves == 0, 1.0, 2.0).astype(jnp.bfloat16)[:, None]
    return jnp.stack([factor * cosine, -(factor * sine)], 0)


def stresses(field):
    trace = (field[0] * field[0] + field[1] * field[1] + field[2] * field[2]) / 3.0
    parts = [
        field[0] * field[0] - trace,
        field[1] * field[1] - trace,
        field[2] * field[2] - trace,
        field[0] * field[1],
        field[0] * field[2],
        field[1] * field[2],
    ]
    return jnp.stack(parts, 0).astype(jnp.bfloat16)


def far_terms(stress, wave_j, axis_one, axis_two, axis_three, y_pos, z_pos):
    points = stress.shape[-1]
    y_count = stress.shape[1]
    z_count = stress.shape[2]
    count = wave_j.shape[0]
    x_pos = jnp.arange(points, dtype=jnp.int32).astype(jnp.float32) * (2.0 * math.pi / points)
    angle_x = wave_j[None, :] * (axis_one[None, :] * x_pos[:, None])
    phase_x = (
        jnp.stack([jnp.cos(angle_x), -jnp.sin(angle_x)], 1)
        .reshape(points, 2 * count)
        .astype(jnp.bfloat16)
    )
    lines = jnp.dot(
        stress.reshape(6 * y_count * z_count, points), phase_x, preferred_element_type=jnp.float32
    )
    lines = lines.reshape(6, y_count, z_count, 2, count)
    weights = [
        axis_one * axis_one,
        axis_two * axis_two,
        axis_three * axis_three,
        2.0 * axis_one * axis_two,
        2.0 * axis_one * axis_three,
        2.0 * axis_two * axis_three,
    ]
    mixed = weights[0][None, None, None, :] * lines[0]
    for index in range(1, 6):
        mixed = mixed + weights[index][None, None, None, :] * lines[index]
    angle = wave_j[None, None, :] * (axis_two[None, None, :] * y_pos[:, None, None]) + wave_j[
        None, None, :
    ] * (axis_three[None, None, :] * z_pos[None, :, None])
    cosine = jnp.cos(angle)
    sine = jnp.sin(angle)
    real_part = mixed[:, :, 0, :]
    imag_part = mixed[:, :, 1, :]
    return jnp.stack(
        [
            jnp.sum(real_part * cosine + imag_part * sine, (0, 1)),
            jnp.sum(imag_part * cosine - real_part * sine, (0, 1)),
        ],
        0,
    )


def body(velocity_modes, wavenumbers, polar, azimuth):
    table = complex_table(M, N)
    table_x = half_table(KX, N)
    rows_kx = velocity_modes.shape[1]
    cols_ky = velocity_modes.shape[2]
    modes = velocity_modes.reshape(3, rows_kx, cols_ky, 2, M)
    first = jnp.einsum(
        "cabpk,pkqz->caqbz", modes, table, preferred_element_type=jnp.float32
    ).astype(jnp.bfloat16)
    moved = lax.all_to_all(first, "col", split_axis=4, concat_axis=3, tiled=True)
    second = jnp.einsum(
        "caqbz,qbpy->cazpy", moved, table, preferred_element_type=jnp.float32
    ).astype(jnp.bfloat16)
    arrived = lax.all_to_all(second, "row", split_axis=4, concat_axis=1, tiled=True)
    field = jnp.einsum("cazpy,pax->cyzx", arrived, table_x, preferred_element_type=jnp.float32)
    velocity = field.astype(jnp.bfloat16)
    stress = stresses(field)
    y_local = field.shape[1]
    z_local = field.shape[2]
    dirs = polar.shape[0]
    wave_j = jnp.repeat(wavenumbers, dirs)
    axis_one = jnp.tile(jnp.sin(polar) * jnp.cos(azimuth), FREQS)
    axis_two = jnp.tile(jnp.sin(polar) * jnp.sin(azimuth), FREQS)
    axis_three = jnp.tile(jnp.cos(polar), FREQS)
    y_index = lax.axis_index("row") * y_local + jnp.arange(y_local, dtype=jnp.int32)
    z_index = lax.axis_index("col") * z_local + jnp.arange(z_local, dtype=jnp.int32)
    y_pos = y_index.astype(jnp.float32) * (2.0 * math.pi / N)
    z_pos = z_index.astype(jnp.float32) * (2.0 * math.pi / N)
    terms = far_terms(stress, wave_j, axis_one, axis_two, axis_three, y_pos, z_pos)
    spectrum = terms.reshape(2, FREQS, dirs) * (wavenumbers * wavenumbers)[None, :, None] / N**1.5
    partial_sum = jnp.transpose(spectrum, (2, 0, 1))
    owned = lax.psum_scatter(partial_sum, "col", scatter_dimension=0, tiled=True)
    far_field = lax.psum(owned, "row")
    return (velocity, far_field)


def solution(mesh):
    return jax.shard_map(
        body,
        mesh=mesh,
        in_specs=(P(None, "row", "col", None), P(), P(), P()),
        out_specs=(P(None, "row", "col", None), P("col", None, None)),
        check_vma=False,
    )
```

profile of v0, /device:TPU:0, one launch (start us, length us, event | category | flops | bytes accessed | tf_op | source)
XLA Modules:
  0.0 1565.9 jit_solution(17726658873091997270)
XLA Ops:
  0.6 20.4 %reshape.626 = bf16[3,44,44,2,352]{4,3,2,1,0:T(2,128)(2,1)} reshape(bf16[3,44,44,704]{3,2,1,0:T(8,128)(2,1)} %param.4) | data formatting | bytes 16355328 | tf_op jit(solution)/shard_map/reshape | solution.py:96
  24.4 17.3 %fusion.7 = bf16[3,44,2,44,512]{4,3,1,0,2:T(8,128)(2,1)} fusion(bf16[3,44,44,2,352]{4,3,2,1,0:T(2,128)(2,1)} %reshape.626, bf16[1,352,2,512]{3,1,0,2:T(8,128)(2,1)S(1)} %get-tuple-element.23, bf16[1,352,2,512]{3,1,0,2:T(8,128)(2,1)S(1)} %get-tuple-element.22), kind=kOutput, calls=%fused_computation.16 | convolution fusion | flops 8382758912 | bytes 21514240 | tf_op jit(solution)/shard_map/cabpk,pkqz->caqbz/dot_general | solution.py:97
  41.7 70.2 %copy.64 = bf16[3,44,2,44,512]{3,2,1,0,4:T(2,128)(2,1)} copy(bf16[3,44,2,44,512]{4,3,1,0,2:T(8,128)(2,1)} %fusion.7) | data formatting | bytes 23789568 | tf_op jit(solution)/shard_map/convert_element_type | solution.py:99
  111.9 118.5 %reshape.636 = bf16[8,2,371712]{2,1,0:T(2,128)(2,1)} reshape(bf16[512,3,44,2,44]{4,3,2,1,0:T(2,128)(2,1)} %bitcast.97) | data formatting | bytes 23789568
  230.3 267.3 %all_to_all.36 = bf16[8,2,371712]{2,1,0:T(2,128)(2,1)} all-to-all(bf16[8,2,371712]{2,1,0:T(2,128)(2,1)} %reshape.636), channel_id=1, replica_groups=mesh['row'=4,'col'=8] {'col'}, dimensions={0} | all-to-all | bytes 23789568 | tf_op jit(solution)/shard_map/all_to_all | solution.py:100
  497.6 126.0 %reshape.637 = bf16[512,3,44,2,44]{4,3,2,1,0:T(2,128)(2,1)} reshape(bf16[8,2,371712]{2,1,0:T(2,128)(2,1)} %all_to_all.36) | data formatting | bytes 23789568
  623.6 23.6 %copy.101 = bf16[3,44,2,44,8,64]{3,4,5,2,1,0:T(8,128)(2,1)} copy(bf16[3,44,2,44,8,64]{3,2,1,0,5,4:T(2,128)(2,1)} %bitcast.98) | data formatting | bytes 23789568 | tf_op jit(solution)/shard_map/all_to_all | solution.py:100
  647.2 44.0 %reshape.630 = bf16[3,44,2,352,64,1]{3,4,2,1,0,5:T(8,128)(2,1)} reshape(bf16[3,44,2,8,44,64]{4,3,5,2,1,0:T(8,128)(2,1)} %bitcast.99) | data formatting | bytes 23789568 | tf_op jit(solution)/shard_map/all_to_all | solution.py:100
  691.2 21.6 %bitcast_convert_fusion = bf16[3,44,64,2,512]{4,2,3,1,0:T(8,128)(2,1)} fusion(bf16[3,44,2,352,64,1]{3,4,2,1,0,5:T(8,128)(2,1)} %reshape.630, bf16[1,352,2,512]{3,1,0,2:T(8,128)(2,1)S(1)} %get-tuple-element.23, bf16[1,352,2,512]{3,1,0,2:T(8,128)(2,1)S(1)} %get-tuple-element.22), kind=kOutput, calls=%fused_computation | convolution fusion | flops 12191793152 | bytes 30638080 | tf_op jit(solution)/shard_map/caqbz,qbpy->cazpy/dot_general | solution.py:101
  712.9 69.9 %copy.67 = bf16[3,44,64,2,512]{2,3,1,0,4:T(2,128)(2,1)} copy(bf16[3,44,64,2,512]{4,2,3,1,0:T(8,128)(2,1)} %bitcast_convert_fusion) | data formatting | bytes 34603008 | tf_op jit(solution)/shard_map/convert_element_type | solution.py:103
  782.7 48.9 %reshape.638 = bf16[4,2,1081344]{2,1,0:T(2,128)(2,1)} reshape(bf16[512,3,44,2,64]{4,3,2,1,0:T(2,128)(2,1)} %bitcast.95) | data formatting | bytes 34603008
  845.7 182.1 %all-to-all-done.1 = bf16[4,2,1081344]{2,1,0:T(2,128)(2,1)} async-done(((bf16[4,2,1081344]{2,1,0:T(2,128)(2,1)}), bf16[4,2,1081344]{2,1,0:T(2,128)(2,1)}, u32[]{:S(2)}, u32[]{:S(2)}) %all-to-all-start.1) | async-done | bytes 17301536 | tf_op jit(solution)/shard_map/all_to_all | solution.py:104
  1027.8 47.9 %reshape.639 = bf16[512,3,44,2,64]{4,3,2,1,0:T(2,128)(2,1)} reshape(bf16[4,2,1081344]{2,1,0:T(2,128)(2,1)} %all-to-all-done.1) | data formatting | bytes 34603008
  1075.7 83.6 %copy.89 = bf16[3,44,64,2,4,128]{5,4,2,3,1,0:T(4,128)(2,1)} copy(bf16[3,44,64,2,4,128]{2,3,1,0,5,4:T(2,128)(2,1)} %bitcast.96) | data formatting | bytes 34603008 | tf_op jit(solution)/shard_map/all_to_all | solution.py:104
  1159.3 15.6 copy.69
  1174.8 33.4 %fusion.53 = (bf16[3,128,64,512]{3,1,2,0:T(8,128)(2,1)}, f32[3,128,64,512]{3,1,2,0:T(8,128)}) fusion(bf16[3,176,64,2,128]{4,2,3,1,0:T(8,128)(2,1)} %bitcast.100, bf16[1,176,512]{2,1,0:T(8,128)(2,1)S(1)} %get-tuple-element.42, bf16[1,176,512]{2,1,0:T(8,128)(2,1)S(1)} %get-tuple-element.41), kind=kOutput, calls=%fused_computation.97 | convolution fusion | flops 8871673856 | bytes 93159424 | tf_op jit(solution)/shard_map/cazpy,pax->cyzx/dot_general | solution.py:105
  1208.3 26.8 %copy.79 = bf16[3,128,64,512]{3,2,1,0:T(8,128)(2,1)} copy(bf16[3,128,64,512]{3,1,2,0:T(8,128)(2,1)} %get-tuple-element.43) | data formatting | bytes 50331648
  1235.1 20.9 %fusion.10 = (bf16[6,128,64,512]{3,1,2,0:T(8,128)(2,1)}, f32[1,128,64,512]{3,1,2,0:T(8,128)S(1)}) fusion(f32[3,128,64,512]{3,1,2,0:T(8,128)} %get-tuple-element.44), kind=kLoop, calls=%fused_computation.17 | loop fusion | flops 33554432 | bytes 75497472
  1255.9 10.9 fusion.11
  1266.9 11.0 fusion.12
  1277.8 15.0 fusion.13
  1292.9 15.1 fusion.14
  1308.0 15.1 fusion.15
  1323.0 45.4 %copy.71 = bf16[6,128,64,512]{3,2,1,0:T(8,128)(2,1)} copy(bf16[6,128,64,512]{3,1,2,0:T(8,128)(2,1)} %fusion.15) | data formatting | bytes 100663296 | tf_op jit(solution)/shard_map/stack | solution.py:45
  1368.5 30.4 %fusion.54 = f32[49152,128]{1,0:T(8,128)} fusion(bf16[49152,512]{1,0:T(8,128)(2,1)} %bitcast.94, bf16[512,128]{0,1:T(8,128)(2,1)S(1)} %bitcast.102), kind=kOutput, calls=%fused_computation.98 | convolution fusion | flops 6442450944 | bytes 75628544 | tf_op jit(solution)/shard_map/dot_general | solution.py:60
  1398.8 17.2 %fusion.51 = (f32[8192,128]{1,0:T(8,128)}, f32[8192,128]{1,0:T(8,128)}, f32[8192,128]{1,0:T(8,128)}, f32[8192,128]{1,0:T(8,128)}, f32[8192,128]{1,0:T(8,128)}, /*index=5*/f32[8192,128]{1,0:T(8,128)}) fusion(f32[49152,128]{1,0:T(8,128)} %fusion.54), kind=kLoop, calls=%fused_computation.95 | loop fusion | bytes 50331648 | tf_op jit(solution)/shard_map/slice | solution.py:72
  1421.6 7.9 squeeze.21
  1448.5 7.9 squeeze.19
  1475.5 7.9 squeeze.17
  1497.0 22.6 %multiply_add_fusion = f32[128,64,2,64]{1,0,3,2:T(8,128)} fusion(f32[128,64,2,64]{1,0,3,2:T(8,128)} %squeeze.21, f32[128,64,2,64]{1,0,3,2:T(8,128)} %squeeze.20, f32[128,64,2,64]{1,0,3,2:T(8,128)} %squeeze.19, f32[128,64,2,64]{1,0,3,2:T(8,128)} %squeeze.18, f32[128,64,2,64]{1,0,3,2:T(8,128)} %squeeze.17, f32[128,64,2,64]{1,0,3,2:T(8,128)} %squeeze.16, ...), kind=kLoop, calls=%fused_computation.23 | loop fusion | flops 11534336 | bytes 29361664 | tf_op jit(solution)/shard_map/add | solution.py:74
  1519.7 19.8 %fusion.21 = (f32[64]{0:T(128)S(1)}, f32[64]{0:T(128)S(1)}) fusion(f32[128,64,2,64]{1,0,3,2:T(8,128)} %multiply_add_fusion, f32[64,64]{0,1:T(8,128)S(1)} %copy-done.1, f32[128,64]{0,1:T(8,128)S(1)} %copy-done.2), kind=kLoop, calls=%fused_computation.31 | loop fusion | flops 4718464 | bytes 4243968 | tf_op jit(solution)/shard_map/reduce_sum | solution.py:84
  1539.8 19.0 %all-reduce = f32[8,2,8]{2,1,0:T(2,128)S(1)} all-reduce(f32[8,2,8]{2,1,0:T(2,128)S(1)} %copy.78), channel_id=2, replica_groups=mesh['row'=4,'col'=8] {'col'}, use_global_device_ids=true, to_apply=%region_2.3.clone | all-reduce | flops 128 | bytes 1024
  (69 shorter events, 82.0 us)
Async XLA Ops:
  831.7 7.5 copy-start.12
  831.7 7.6 copy-start.11
  831.7 7.7 copy-start.9
  831.7 8.6 copy-start.13
  831.7 196.1 %all-to-all-start.1 = ((bf16[4,2,1081344]{2,1,0:T(2,128)(2,1)}), bf16[4,2,1081344]{2,1,0:T(2,128)(2,1)}, u32[]{:S(2)}, u32[]{:S(2)}) async-start(bf16[4,2,1081344]{2,1,0:T(2,128)(2,1)} %reshape.638), calls=%async_computation.1 | async-start | bytes 34603008 | tf_op jit(solution)/shard_map/all_to_all | solution.py:104
  1323.0 45.4 %copy-start = (bf16[512,2,64]{0,2,1:T(8,128)(2,1)S(1)}, bf16[512,2,64]{0,2,1:T(8,128)(2,1)}, u32[]{:S(2)}) copy-start(bf16[512,2,64]{0,2,1:T(8,128)(2,1)} %pad_maximum_fusion.3) | copy-start | bytes 393220
  1483.3 13.7 copy-start.3
  1483.3 13.7 copy-start.4
  1483.3 13.7 copy-start.5
  1483.3 13.7 copy-start.6
  1483.3 13.7 copy-start.7
  1483.3 13.7 copy-start.8
  1497.0 22.7 %copy-start.1 = (f32[64,64]{0,1:T(8,128)S(1)}, f32[64,64]{0,1:T(8,128)}, u32[]{:S(2)}) copy-start(f32[64,64]{0,1:T(8,128)} %multiply_multiply_fusion.1) | copy-start | bytes 49156
  1497.0 22.7 %copy-start.2 = (f32[128,64]{0,1:T(8,128)S(1)}, f32[128,64]{0,1:T(8,128)}, u32[]{:S(2)}) copy-start(f32[128,64]{0,1:T(8,128)} %multiply_multiply_fusion.2) | copy-start | bytes 98308
  1497.0 42.6 %copy-start.10 = (f32[8]{0:T(128)S(1)}, f32[8]{0:T(128)}, u32[]{:S(2)}) copy-start(f32[8]{0:T(128)} %mul.534) | copy-start | bytes 100
where the time goes:
time: 1580 us; the launch traced here: 1570 us
  local copies, waits for them, and re-layouts  841 us (53%)
  blocking collectives  293 us (19%)
  waiting for transfers between devices  182 us (12%)
  other arithmetic  139 us (9%)
  matrix products  103 us (7%)
    unnamed x35, local copies, waits for them, and re-layouts  369 us
    all_to_all x1, blocking collectives, body(): lax.all_to_all(first, 'col', split_axis=4, concat_axis=3, tiled=True)  267 us
    all_to_all x1, waiting for transfers between devices, body(): lax.all_to_all(second, 'row', split_axis=4, concat_axis=1, tiled=True)  182 us
    all_to_all x2, local copies, waits for them, and re-layouts, body(): lax.all_to_all(second, 'row', split_axis=4, concat_axis=1, tiled=True)  99.1 us
    unnamed x5, other arithmetic  72.9 us
    convert_element_type x1, local copies, waits for them, and re-layouts, body(): first = jnp.einsum('cabpk,pkqz->caqbz', modes, table, preferred_element_t...  70.2 us
    convert_element_type x1, local copies, waits for them, and re-layouts, body(): second = jnp.einsum('caqbz,qbpy->cazpy', moved, table, preferred_element_...  69.9 us
    all_to_all x2, local copies, waits for them, and re-layouts, body(): lax.all_to_all(first, 'col', split_axis=4, concat_axis=3, tiled=True)  67.6 us
  transfers between devices with their start and end apart: 1, of which 1 were waited for; matrix products, arithmetic and copies ran while one was open for 0% of the time, Pallas kernels for 0%

commit v1 on v0

--- a/solution.py
+++ b/solution.py
@@ -101,7 +101,10 @@
     second = jnp.einsum(
         "caqbz,qbpy->cazpy", moved, table, preferred_element_type=jnp.float32
     ).astype(jnp.bfloat16)
-    arrived = lax.all_to_all(second, "row", split_axis=4, concat_axis=1, tiled=True)
+    n_dev = lax.axis_size("row")
+    blocks = jnp.stack(jnp.split(second, n_dev, axis=4), axis=0)
+    blocks = lax.all_to_all(blocks, "row", split_axis=0, concat_axis=0)
+    arrived = jnp.concatenate(blocks, axis=1)
     field = jnp.einsum("cazpy,pax->cyzx", arrived, table_x, preferred_element_type=jnp.float32)
     velocity = field.astype(jnp.bfloat16)
     stress = stresses(field)

time: 1580 us -> 1340 us (0.85)
  local copies, waits for them, and re-layouts: 841 us -> 600 us
    all_to_all x2 -> x0, local copies, waits for them, and re-layouts: 99.1 us -> none  [body(): lax.all_to_all(second, 'row', split_axis=4, concat_axis=1, tiled=True)]
    unnamed x35 -> x33, local copies, waits for them, and re-layouts: 369 us -> 272 us
    convert_element_type x1 -> x0, local copies, waits for them, and re-layouts: 69.9 us -> none  [body(): second = jnp.einsum('caqbz,qbpy->cazpy', moved, table, preferred_element_...]
    reshape x0 -> x1, local copies, waits for them, and re-layouts: none -> 16.4 us  [body(): arrived = jnp.concatenate(blocks, axis=1)]
where the time goes in v1:
time: 1340 us; the launch traced here: 1330 us
  local copies, waits for them, and re-layouts  600 us (45%)
  blocking collectives  293 us (22%)
  waiting for transfers between devices  182 us (14%)
  other arithmetic  147 us (11%)
  matrix products  102 us (8%)
    unnamed x33, local copies, waits for them, and re-layouts  272 us
    all_to_all x1, blocking collectives, body(): lax.all_to_all(first, 'col', split_axis=4, concat_axis=3, tiled=True)  268 us
    all_to_all x1, waiting for transfers between devices, body(): blocks = lax.all_to_all(blocks, 'row', split_axis=0, concat_axis=0)  182 us
    unnamed x5, other arithmetic  73.1 us
    convert_element_type x1, local copies, waits for them, and re-layouts, body(): first = jnp.einsum('cabpk,pkqz->caqbz', modes, table, preferred_element_t...  70.1 us
    all_to_all x2, local copies, waits for them, and re-layouts, body(): lax.all_to_all(first, 'col', split_axis=4, concat_axis=3, tiled=True)  67.6 us
    another operation x1, local copies, waits for them, and re-layouts, stresses(): return jnp.stack(parts, 0).astype(jnp.bfloat16)  45.5 us
    squeeze x5, local copies, waits for them, and re-layouts, far_terms(): mixed = mixed + weights[index][None, None, None, :] * lines[index]  39.5 us
  transfers between devices with their start and end apart: 1, of which 1 were waited for; matrix products, arithmetic and copies ran while one was open for 0% of the time, Pallas kernels for 0%

profile of v1, /device:TPU:0, one launch (start us, length us, event | category | flops | bytes accessed | tf_op | source)
XLA Modules:
  0.0 1331.8 jit_solution(10194990814005087646)
XLA Ops:
  0.6 20.4 %reshape.632 = bf16[3,44,44,2,352]{4,3,2,1,0:T(2,128)(2,1)} reshape(bf16[3,44,44,704]{3,2,1,0:T(8,128)(2,1)} %param.4) | data formatting | bytes 16355328 | tf_op jit(solution)/shard_map/reshape | solution.py:96
  24.4 17.3 %fusion.7 = bf16[3,44,2,44,512]{4,3,1,0,2:T(8,128)(2,1)} fusion(bf16[3,44,44,2,352]{4,3,2,1,0:T(2,128)(2,1)} %reshape.632, bf16[1,352,2,512]{3,1,0,2:T(8,128)(2,1)S(1)} %get-tuple-element.25, bf16[1,352,2,512]{3,1,0,2:T(8,128)(2,1)S(1)} %get-tuple-element.24), kind=kOutput, calls=%fused_computation.17 | convolution fusion | flops 8382758912 | bytes 21514240 | tf_op jit(solution)/shard_map/cabpk,pkqz->caqbz/dot_general | solution.py:97
  41.7 70.1 %copy.45 = bf16[3,44,2,44,512]{3,2,1,0,4:T(2,128)(2,1)} copy(bf16[3,44,2,44,512]{4,3,1,0,2:T(8,128)(2,1)} %fusion.7) | data formatting | bytes 23789568 | tf_op jit(solution)/shard_map/convert_element_type | solution.py:99
  111.8 118.5 %reshape.644 = bf16[8,2,371712]{2,1,0:T(2,128)(2,1)} reshape(bf16[512,3,44,2,44]{4,3,2,1,0:T(2,128)(2,1)} %bitcast.100) | data formatting | bytes 23789568
  230.3 267.5 %all_to_all.23 = bf16[8,2,371712]{2,1,0:T(2,128)(2,1)} all-to-all(bf16[8,2,371712]{2,1,0:T(2,128)(2,1)} %reshape.644), channel_id=1, replica_groups=mesh['row'=4,'col'=8] {'col'}, dimensions={0} | all-to-all | bytes 23789568 | tf_op jit(solution)/shard_map/all_to_all | solution.py:100
  497.8 126.0 %reshape.645 = bf16[512,3,44,2,44]{4,3,2,1,0:T(2,128)(2,1)} reshape(bf16[8,2,371712]{2,1,0:T(2,128)(2,1)} %all_to_all.23) | data formatting | bytes 23789568
  623.8 23.6 %copy.79 = bf16[3,44,2,44,8,64]{3,4,5,2,1,0:T(8,128)(2,1)} copy(bf16[3,44,2,44,8,64]{3,2,1,0,5,4:T(2,128)(2,1)} %bitcast.101) | data formatting | bytes 23789568 | tf_op jit(solution)/shard_map/all_to_all | solution.py:100
  647.4 44.0 %reshape.638 = bf16[3,44,2,352,64,1]{3,4,2,1,0,5:T(8,128)(2,1)} reshape(bf16[3,44,2,8,44,64]{4,3,5,2,1,0:T(8,128)(2,1)} %bitcast.102) | data formatting | bytes 23789568 | tf_op jit(solution)/shard_map/all_to_all | solution.py:100
  691.4 21.2 %bitcast_convert_fusion = bf16[3,44,64,2,512]{4,2,3,1,0:T(8,128)(2,1)} fusion(bf16[3,44,2,352,64,1]{3,4,2,1,0,5:T(8,128)(2,1)} %reshape.638, bf16[1,352,2,512]{3,1,0,2:T(8,128)(2,1)S(1)} %get-tuple-element.25, bf16[1,352,2,512]{3,1,0,2:T(8,128)(2,1)S(1)} %get-tuple-element.24), kind=kOutput, calls=%fused_computation | convolution fusion | flops 12191793152 | bytes 30638080 | tf_op jit(solution)/shard_map/caqbz,qbpy->cazpy/dot_general | solution.py:101
  712.6 8.3 slice_bitcast_fusion.3
  742.0 182.2 %all-to-all-done.1 = bf16[4,3,44,64,2,128]{5,3,4,2,1,0:T(8,128)(2,1)} async-done(((bf16[4,3,44,64,2,128]{5,3,4,2,1,0:T(8,128)(2,1)}), bf16[4,3,44,64,2,128]{5,3,4,2,1,0:T(8,128)(2,1)}, u32[]{:S(2)}, u32[]{:S(2)}) %all-to-all-start.1) | async-done | bytes 17301536 | tf_op jit(solution)/shard_map/all_to_all | solution.py:106
  924.1 16.4 %copy.48 = bf16[3,4,44,64,2,128]{5,3,4,2,1,0:T(8,128)(2,1)} copy(bf16[3,4,44,64,2,128]{5,3,4,2,0,1:T(8,128)(2,1)} %bitcast.22) | data formatting | bytes 34603008 | tf_op jit(solution)/shard_map/reshape | solution.py:107
  940.5 33.4 %fusion.53 = (bf16[3,128,64,512]{3,1,2,0:T(8,128)(2,1)}, f32[3,128,64,512]{3,1,2,0:T(8,128)}) fusion(bf16[3,176,64,2,128]{4,2,3,1,0:T(8,128)(2,1)} %bitcast.103, bf16[1,176,512]{2,1,0:T(8,128)(2,1)S(1)} %get-tuple-element.44, bf16[1,176,512]{2,1,0:T(8,128)(2,1)S(1)} %get-tuple-element.43), kind=kOutput, calls=%fused_computation.102 | convolution fusion | flops 8871673856 | bytes 93159424 | tf_op jit(solution)/shard_map/cazpy,pax->cyzx/dot_general | solution.py:108
  974.0 26.6 %copy.58 = bf16[3,128,64,512]{3,2,1,0:T(8,128)(2,1)} copy(bf16[3,128,64,512]{3,1,2,0:T(8,128)(2,1)} %get-tuple-element.45) | data formatting | bytes 50331648
  1000.6 20.9 %fusion.10 = (bf16[6,128,64,512]{3,1,2,0:T(8,128)(2,1)}, f32[1,128,64,512]{3,1,2,0:T(8,128)S(1)}) fusion(f32[3,128,64,512]{3,1,2,0:T(8,128)} %get-tuple-element.46), kind=kLoop, calls=%fused_computation.18 | loop fusion | flops 33554432 | bytes 75497472
  1021.5 10.9 fusion.11
  1032.4 11.2 fusion.12
  1043.5 15.1 %fusion.13 = bf16[6,128,64,512]{3,1,2,0:T(8,128)(2,1)} fusion(bf16[6,128,64,512]{3,1,2,0:T(8,128)(2,1)} %fusion.12, f32[3,128,64,512]{3,1,2,0:T(8,128)} %get-tuple-element.46), kind=kLoop, calls=%fused_computation.21 | loop fusion | flops 8388608 | bytes 41943040
  1058.6 15.1 %fusion.14 = bf16[6,128,64,512]{3,1,2,0:T(8,128)(2,1)} fusion(bf16[6,128,64,512]{3,1,2,0:T(8,128)(2,1)} %fusion.13, f32[3,128,64,512]{3,1,2,0:T(8,128)} %get-tuple-element.46), kind=kLoop, calls=%fused_computation.22 | loop fusion | flops 8388608 | bytes 41943040
  1073.7 15.1 %fusion.15 = bf16[6,128,64,512]{3,1,2,0:T(8,128)(2,1)} fusion(bf16[6,128,64,512]{3,1,2,0:T(8,128)(2,1)} %fusion.14, f32[3,128,64,512]{3,1,2,0:T(8,128)} %get-tuple-element.46), kind=kLoop, calls=%fused_computation.23 | loop fusion | flops 8388608 | bytes 41943040 | tf_op jit(solution)/shard_map/stack | solution.py:45
  1088.7 45.5 %copy.50 = bf16[6,128,64,512]{3,2,1,0:T(8,128)(2,1)} copy(bf16[6,128,64,512]{3,1,2,0:T(8,128)(2,1)} %fusion.15) | data formatting | bytes 100663296 | tf_op jit(solution)/shard_map/stack | solution.py:45
  1134.2 30.0 %fusion.54 = f32[49152,128]{1,0:T(8,128)} fusion(bf16[49152,512]{1,0:T(8,128)(2,1)} %bitcast.99, bf16[512,128]{0,1:T(8,128)(2,1)S(1)} %bitcast.104), kind=kOutput, calls=%fused_computation.103 | convolution fusion | flops 6442450944 | bytes 75628544 | tf_op jit(solution)/shard_map/dot_general | solution.py:60
  1164.2 17.2 %fusion.51 = (f32[8192,128]{1,0:T(8,128)}, f32[8192,128]{1,0:T(8,128)}, f32[8192,128]{1,0:T(8,128)}, f32[8192,128]{1,0:T(8,128)}, f32[8192,128]{1,0:T(8,128)}, /*index=5*/f32[8192,128]{1,0:T(8,128)}) fusion(f32[49152,128]{1,0:T(8,128)} %fusion.54), kind=kLoop, calls=%fused_computation.100 | loop fusion | bytes 50331648 | tf_op jit(solution)/shard_map/slice | solution.py:72
  1187.0 8.1 squeeze.21
  1200.8 7.8 squeeze.20
  1214.2 7.9 squeeze.19
  1227.7 7.8 squeeze.18
  1241.2 7.9 squeeze.17
  1254.7 7.8 squeeze.16
  1262.6 22.6 %multiply_add_fusion = f32[128,64,2,64]{1,0,3,2:T(8,128)} fusion(f32[128,64,2,64]{1,0,3,2:T(8,128)} %squeeze.21, f32[128,64,2,64]{1,0,3,2:T(8,128)} %squeeze.20, f32[128,64,2,64]{1,0,3,2:T(8,128)} %squeeze.19, f32[128,64,2,64]{1,0,3,2:T(8,128)} %squeeze.18, f32[128,64,2,64]{1,0,3,2:T(8,128)} %squeeze.17, f32[128,64,2,64]{1,0,3,2:T(8,128)} %squeeze.16, ...), kind=kLoop, calls=%fused_computation.24 | loop fusion | flops 11534336 | bytes 29361664 | tf_op jit(solution)/shard_map/add | solution.py:74
  1285.3 19.8 %fusion.21 = (f32[64]{0:T(128)S(1)}, f32[64]{0:T(128)S(1)}) fusion(f32[128,64,2,64]{1,0,3,2:T(8,128)} %multiply_add_fusion, f32[64,64]{0,1:T(8,128)S(1)} %copy-done.1, f32[128,64]{0,1:T(8,128)S(1)} %copy-done.2), kind=kLoop, calls=%fused_computation.36 | loop fusion | flops 4718464 | bytes 4243968 | tf_op jit(solution)/shard_map/reduce_sum | solution.py:84
  1305.4 19.1 %all-reduce = f32[8,2,8]{2,1,0:T(2,128)S(1)} all-reduce(f32[8,2,8]{2,1,0:T(2,128)S(1)} %copy.57), channel_id=2, replica_groups=mesh['row'=4,'col'=8] {'col'}, use_global_device_ids=true, to_apply=%region_2.3.clone | all-reduce | flops 128 | bytes 1024
  (67 shorter events, 65.3 us)
Async XLA Ops:
  728.1 7.4 copy-start.12
  728.1 7.5 copy-start.11
  728.1 7.6 copy-start.9
  728.1 8.5 copy-start.13
  728.1 196.0 %all-to-all-start.1 = ((bf16[4,3,44,64,2,128]{5,3,4,2,1,0:T(8,128)(2,1)}), bf16[4,3,44,64,2,128]{5,3,4,2,1,0:T(8,128)(2,1)}, u32[]{:S(2)}, u32[]{:S(2)}) async-start(bf16[4,3,44,64,2,128]{5,3,4,2,1,0:T(8,128)(2,1)} %pad_maximum_fusion), calls=%async_computation.1 | async-start | bytes 34603008 | tf_op jit(solution)/shard_map/all_to_all | solution.py:106
  1088.7 45.5 %copy-start = (bf16[512,2,64]{0,2,1:T(8,128)(2,1)S(1)}, bf16[512,2,64]{0,2,1:T(8,128)(2,1)}, u32[]{:S(2)}) copy-start(bf16[512,2,64]{0,2,1:T(8,128)(2,1)} %pad_maximum_fusion.4) | copy-start | bytes 393220
  1249.0 13.5 %copy-start.3 = (f32[64]{0:T(128)S(1)}, f32[64]{0:T(128)}, u32[]{:S(2)}) copy-start(f32[64]{0:T(128)} %get-tuple-element.31) | copy-start | bytes 772
  1249.0 13.5 %copy-start.4 = (f32[64]{0:T(128)S(1)}, f32[64]{0:T(128)}, u32[]{:S(2)}) copy-start(f32[64]{0:T(128)} %get-tuple-element.32) | copy-start | bytes 772
  1249.0 13.5 %copy-start.5 = (f32[64]{0:T(128)S(1)}, f32[64]{0:T(128)}, u32[]{:S(2)}) copy-start(f32[64]{0:T(128)} %get-tuple-element.33) | copy-start | bytes 772
  1249.0 13.5 %copy-start.6 = (f32[64]{0:T(128)S(1)}, f32[64]{0:T(128)}, u32[]{:S(2)}) copy-start(f32[64]{0:T(128)} %get-tuple-element.38) | copy-start | bytes 772
  1249.0 13.5 %copy-start.7 = (f32[64]{0:T(128)S(1)}, f32[64]{0:T(128)}, u32[]{:S(2)}) copy-start(f32[64]{0:T(128)} %get-tuple-element.39) | copy-start | bytes 772
  1249.1 13.5 %copy-start.8 = (f32[64]{0:T(128)S(1)}, f32[64]{0:T(128)}, u32[]{:S(2)}) copy-start(f32[64]{0:T(128)} %get-tuple-element.40) | copy-start | bytes 772
  1262.6 22.7 %copy-start.1 = (f32[64,64]{0,1:T(8,128)S(1)}, f32[64,64]{0,1:T(8,128)}, u32[]{:S(2)}) copy-start(f32[64,64]{0,1:T(8,128)} %multiply_multiply_fusion.1) | copy-start | bytes 49156
  1262.6 22.7 %copy-start.2 = (f32[128,64]{0,1:T(8,128)S(1)}, f32[128,64]{0,1:T(8,128)}, u32[]{:S(2)}) copy-start(f32[128,64]{0,1:T(8,128)} %multiply_multiply_fusion.2) | copy-start | bytes 98308
  1262.6 42.6 %copy-start.10 = (f32[8]{0:T(128)S(1)}, f32[8]{0:T(128)}, u32[]{:S(2)}) copy-start(f32[8]{0:T(128)} %mul.534) | copy-start | bytes 100
